TPU v7x, 32 devices: a whole 2x2x4 slice. The times are simulated.
32 devices in a mesh: ta: 4 (over y, core), gx: 2 (over x), gy: 4 (over z).
Axes of the slice: x: 2, y: 2, z: 4, core: 2. Of those that a mesh axis runs over, the one named last changes fastest.
Arguments:
- space_links: float32 [3, 2, 3, 3, 4, 4, 2304], P(None, None, None, None, 'ta', 'gx', 'gy'), may hold values from -1 to 1, as said below
- time_links: float32 [2, 3, 3, 4, 4, 2304], P(None, None, None, 'ta', 'gx', 'gy'), may hold values from -1 to 1, as said below
- start_gauge: float32 [2, 3, 3, 4, 4, 2304], P(None, None, None, 'ta', 'gx', 'gy'), may hold values from -1 to 1, as said below
Outputs:
- gauge_field: float32 [2, 3, 3, 4, 4, 2304], P(None, None, None, 'ta', 'gx', 'gy')
- time_rotated: float32 [2, 3, 3, 4, 4, 2304], P(None, None, None, 'ta', 'gx', 'gy')
- functional: float32 [4, 4], P(None, 'ta')
- theta: float32 [4], P('ta')
Inputs may be any that keep to these rules, and one draw needn't show every extreme that they name: `space_links`: at every site the matrix is special unitary. `time_links`: at every site the matrix is special unitary. `start_gauge`: at every site the matrix is special unitary.
All inputs are finite; a program needn't handle non-finite values.
Results may differ from a plain program's by a relative error of at most 0.00021.
Values sent between devices are 32-bit elements; how exact they have to be, the bound alone decides.
A program may use at most 64 MiB of HBM per device.

v0:
```python
import functools

import jax
import jax.numpy as jnp
from jax import lax
from jax.experimental import pallas as pl
from jax.experimental.pallas import tpu as pltpu
from jax.sharding import PartitionSpec as P

NZ = 48
ITERS = 4
OMEGA = 1.7
FLOOR = 0.5
PAIRS = ((0, 1), (1, 2), (0, 2))

COMPS = 72
GAUGE = 54
MESH = pl.DeviceIdType.MESH


def tile(ref, row):
    return ref[pl.ds(row * 8, 8), :]


def z_shift(v, masks, step):
    lane, z = masks
    if step > 0:
        return jnp.where(z == NZ - 1, pltpu.roll(v, NZ - 1, 1), pltpu.roll(v, 127, 1))
    return jnp.where(z == 0, pltpu.roll(v, 128 - (NZ - 1), 1), pltpu.roll(v, 1, 1))


def y_shift(v, masks, step):
    lane, z = masks
    swapped = pltpu.roll(v, 64, 1)
    if step > 0:
        return jnp.where(lane < 64, swapped, pltpu.roll(swapped, 7, 0))
    return jnp.where(lane >= 64, swapped, pltpu.roll(swapped, 1, 0))


def add_links_times_dagger(total, u, g):
    for i in range(3):
        for j in range(3):
            re, im = total[i * 3 + j], total[9 + i * 3 + j]
            for k in range(3):
                ur, ui = u[i * 3 + k], u[9 + i * 3 + k]
                gr, gi = g[j * 3 + k], g[9 + j * 3 + k]
                tr = ur * gr + ui * gi
                ti = ui * gr - ur * gi
                re = tr if re is None else re + tr
                im = ti if im is None else im + ti
            total[i * 3 + j], total[9 + i * 3 + j] = re, im


def add_dagger_times_dagger(total, v, g):
    for i in range(3):
        for j in range(3):
            re, im = total[i * 3 + j], total[9 + i * 3 + j]
            for k in range(3):
                vr, vi = v[k * 3 + i], v[9 + k * 3 + i]
                gr, gi = g[j * 3 + k], g[9 + j * 3 + k]
                tr = vr * gr - vi * gi
                ti = vr * gi + vi * gr
                re = tr if re is None else re + tr
                im = -ti if im is None else im - ti
            total[i * 3 + j], total[9 + i * 3 + j] = re, im


def times(a, b):
    out = [None] * 18
    for i in range(3):
        for j in range(3):
            re = im = None
            for k in range(3):
                ar, ai = a[i * 3 + k], a[9 + i * 3 + k]
                br, bi = b[k * 3 + j], b[9 + k * 3 + j]
                tr = ar * br - ai * bi
                ti = ar * bi + ai * br
                re = tr if re is None else re + tr
                im = ti if im is None else im + ti
            out[i * 3 + j], out[9 + i * 3 + j] = re, im
    return out


def turn(m, i, j, a):
    out = list(m)
    for col in range(3):
        fr, fi = m[i * 3 + col], m[9 + i * 3 + col]
        sr, si = m[j * 3 + col], m[9 + j * 3 + col]
        out[i * 3 + col] = (a[0] * fr - a[3] * fi) + (a[2] * sr - a[1] * si)
        out[9 + i * 3 + col] = (a[0] * fi + a[3] * fr) + (a[2] * si + a[1] * sr)
        out[j * 3 + col] = (a[0] * sr + a[3] * si) - (a[2] * fr + a[1] * fi)
        out[9 + j * 3 + col] = (a[0] * si - a[3] * sr) - (a[2] * fi - a[1] * fr)
    return out


def relax(g, m):
    for i, j in PAIRS:
        c0 = m[i * 3 + i] + m[j * 3 + j]
        c1 = -(m[9 + i * 3 + j] + m[9 + j * 3 + i])
        c2 = m[j * 3 + i] - m[i * 3 + j]
        c3 = m[9 + j * 3 + j] - m[9 + i * 3 + i]
        length = jnp.sqrt(c0 * c0 + c1 * c1 + c2 * c2 + c3 * c3)
        v0 = (1.0 - OMEGA) * length + OMEGA * c0
        v1, v2, v3 = OMEGA * c1, OMEGA * c2, OMEGA * c3
        inverse = jnp.minimum(lax.rsqrt(v0 * v0 + v1 * v1 + v2 * v2 + v3 * v3), 1.0 / FLOOR)
        a = [v0 * inverse, v1 * inverse, v2 * inverse, v3 * inverse]
        g = turn(g, i, j, a)
        m = turn(m, i, j, a)
    return g, m


def squares(m):
    total = None
    for i, j in ((0, 1), (0, 2), (1, 2)):
        a = m[i * 3 + j] - m[j * 3 + i]
        b = m[9 + i * 3 + j] + m[9 + j * 3 + i]
        term = 0.5 * (a * a + b * b)
        total = term if total is None else total + term
    third = (m[9] + m[13] + m[17]) * (1.0 / 3.0)
    for i in (9, 13, 17):
        d = m[i] - third
        total = total + d * d
    return total


def kernel(
    sizes, raw_ref, time_ref, out_ref, sums_ref,
    raw_in, field, back, edge_out, edge_in, step_out, step_in, full_in,
    time_links, time_in, rotated, parts, total_out, total_in,
    raw_sems, edge_sems, step_sems, full_sems, time_sems, total_sems,
):
    n_t, n_x, n_y = sizes
    ring = n_x == 2
    offsets = (0, 1) if ring else (0, n_x - 1, 1)
    slots = len(offsets)
    ahead = [offsets.index((d + 1) % n_x) if (d + 1) % n_x in offsets else p for p, d in enumerate(offsets)]
    behind = [offsets.index((d - 1) % n_x) if (d - 1) % n_x in offsets else p for p, d in enumerate(offsets)]
    t, x, y = lax.axis_index("ta"), lax.axis_index("gx"), lax.axis_index("gy")

    def device(dt, dx, dy):
        return {
            "ta": lax.rem(t + dt % n_t, n_t),
            "gx": lax.rem(x + dx % n_x, n_x),
            "gy": lax.rem(y + dy % n_y, n_y),
        }

    def remote(src, dst, sems, index, dt, dx, dy):
        return pltpu.make_async_remote_copy(
            src_ref=src,
            dst_ref=dst,
            send_sem=sems.at[(0,) + index],
            recv_sem=sems.at[(1,) + index],
            device_id=device(dt, dx, dy),
            device_id_type=MESH,
        )

    peers = [(0, dx, dy) for dx in range(n_x) for dy in range(n_y) if dx or dy]
    greet = peers + [(1, 0, 0), (n_t - 1, 0, 0)]
    barrier = pltpu.get_barrier_semaphore()
    for peer in greet:
        pl.semaphore_signal(barrier, inc=1, device_id=device(*peer), device_id_type=MESH)

    lane = lax.broadcasted_iota(jnp.int32, (8, 128), 1)
    row = lax.broadcasted_iota(jnp.int32, (8, 128), 0)
    z = lax.rem(lane, 64)
    masks = (lane, z)
    first_plane = [lax.rem(lane + lax.div(lane, 64) + u, 2) == 0 for u in (0, 1)]
    counted = (row >= 1) & (row <= 6) & (z < NZ)

    def spread_row(ref, rows, s):
        lanes = lax.broadcasted_iota(jnp.int32, (rows, 128), 1)
        start = 2 * NZ * s
        number, off = start // 128, start % 128
        low = ref[:, number * 128 : number * 128 + 128]
        high = ref[:, number * 128 + 128 : number * 128 + 256] if off + 2 * NZ > 128 else None

        def window(shift):
            one = pltpu.roll(low, (-shift) % 128, 1)
            if high is None:
                return one
            return jnp.where(lanes + shift < 128, one, pltpu.roll(high, (-shift) % 128, 1))

        return jnp.where(lanes < 64, window(off), window(off + NZ - 64))

    rows = 2 * COMPS
    last = 6
    edge_low = spread_row(raw_ref, rows, 0)
    edge_high = spread_row(raw_ref, rows, last - 1)
    edge_out[0] = edge_low
    edge_out[1] = edge_high
    own = field.at[0]
    own[pl.ds(1, rows, stride=8), :] = edge_low
    own[pl.ds(last, rows, stride=8), :] = edge_high

    pl.semaphore_wait(barrier, len(greet))
    first_copies = []
    for p, d in enumerate(offsets):
        if d:
            first_copies.append(remote(raw_ref, raw_in.at[p - 1], raw_sems, (p - 1,), 0, -d, 0))
            first_copies[-1].start()
    edge_copies = []
    for p, d in enumerate(offsets):
        for way in (0, 1):
            edge_copies.append(
                remote(edge_out.at[way], edge_in.at[p, way], edge_sems, (p, way), 0, -d, (-1, 1)[way])
            )
            edge_copies[-1].start()

    for s in range(1, last - 1):
        own[pl.ds(s + 1, rows, stride=8), :] = spread_row(raw_ref, rows, s)
    for s in range(6):
        time_links[pl.ds(s + 1, 40, stride=8), :] = spread_row(time_ref, 40, s)
    for copy in first_copies:
        copy.wait_recv()
    for p in range(1, slots):
        for s in range(last):
            field.at[p][pl.ds(s + 1, rows, stride=8), :] = spread_row(raw_in.at[p - 1], rows, s)
    for copy in edge_copies:
        copy.wait_recv()
    for p in range(slots):
        field.at[p][pl.ds(7, rows, stride=8), :] = edge_in[p, 0]
        field.at[p][pl.ds(0, rows, stride=8), :] = edge_in[p, 1]

    def matrix(p, colour, base):
        return [tile(field.at[p], colour * COMPS + base + c) for c in range(18)]

    def neighbour(p, colour, base, c, direction, step):
        at = (1 - colour) * COMPS + base + c
        here = tile(field.at[p], at)
        if direction == 2:
            return z_shift(here, masks, step)
        if direction == 1:
            return y_shift(here, masks, step)
        if step > 0:
            return jnp.where(first_plane[colour], here, tile(field.at[ahead[p]], at))
        return jnp.where(first_plane[colour], tile(field.at[behind[p]], at), here)

    for p in range(slots):
        for direction in range(3):
            for colour in (0, 1):
                for c in range(18):
                    value = neighbour(p, colour, direction * 18, c, direction, -1)
                    back[p, pl.ds((((direction * 2) + colour) * 18 + c) * 8, 8), :] = value

    def staple(p, colour):
        total = [None] * 18
        for direction in range(3):
            u = matrix(p, colour, direction * 18)
            g = [neighbour(p, colour, GAUGE, c, direction, 1) for c in range(18)]
            add_links_times_dagger(total, u, g)
            v = [tile(back.at[p], (direction * 2 + colour) * 18 + c) for c in range(18)]
            g = [neighbour(p, colour, GAUGE, c, direction, -1) for c in range(18)]
            add_dagger_times_dagger(total, v, g)
        return total

    def half(p, colour):
        g, m = relax(matrix(p, colour, GAUGE), times(matrix(p, colour, GAUGE), staple(p, colour)))
        return g, m

    def store(p, colour, g):
        for c in range(18):
            field[p, pl.ds((colour * COMPS + GAUGE + c) * 8, 8), :] = g[c]

    summed = range(slots) if ring else range(1)

    def gauge_rows(p, colour):
        return field.at[p, pl.ds((colour * COMPS + GAUGE) * 8, 18 * 8), :]

    def time_copy(colour):
        return remote(gauge_rows(0, colour), time_in.at[colour], time_sems, (colour,), -1, 0, 0)

    def step_copies(k):
        copies = []
        if ring:
            for way in (0, 1):
                copies.append(
                    remote(
                        step_out.at[k, way], step_in.at[k, 0, way], step_sems, (k, 0, way), 0, 0, (-1, 1)[way]
                    )
                )
        else:
            for p, d in enumerate(offsets):
                for way in (0, 1):
                    copies.append(
                        remote(
                            step_out.at[k, way], step_in.at[k, p, way], step_sems, (k, p, way),
                            0, -d, (-1, 1)[way],
                        )
                    )
                if d:
                    copies.append(
                        remote(gauge_rows(0, 1), full_in.at[k, p - 1], full_sems, (k, p - 1), 0, -d, 0)
                    )
        return copies

    def iteration(k, carry):
        for p in range(slots):
            g, m = half(p, 0)
            store(p, 0, g)

        @pl.when(k == ITERS - 1)
        def _():
            time_copy(0).start()

        trace = None
        square = None
        for p in range(slots):
            g, m = half(p, 1)
            store(p, 1, g)
            if p in summed:
                one = m[0] + m[4] + m[8]
                trace = one if trace is None else trace + one
                two = squares(m)
                square = two if square is None else square + two
        parts[k] = jnp.where(counted, trace, 0.0)
        parts[ITERS] = jnp.where(counted, square, 0.0)
        base = (COMPS + GAUGE) * 8
        for p in summed:
            for way in (0, 1):
                edge = field.at[p][pl.ds(base + (1, last)[way], 18, stride=8), :]
                step_out[k, way, p] = edge
        copies = step_copies(k)
        for copy in copies:
            copy.start()

        for copy in copies:
            copy.wait_send()
        for copy in copies:
            copy.wait_recv()
        if not ring:
            for p in range(1, slots):
                field[p, pl.ds(base, 144), :] = full_in[k, p - 1]
        for p in range(slots):
            source = (0, p) if ring else (p, 0)
            field.at[p][pl.ds(base + 7, 18, stride=8), :] = step_in[k, source[0], 0, source[1]]
            field.at[p][pl.ds(base, 18, stride=8), :] = step_in[k, source[0], 1, source[1]]
        return carry

    lax.fori_loop(0, ITERS, iteration, 0)
    time_copy(1).start()

    square = None
    for p in summed:
        two = squares(times(matrix(p, 0, GAUGE), staple(p, 0)))
        square = two if square is None else square + two
    parts[ITERS] = parts[ITERS] + jnp.where(counted, square, 0.0)
    block = jnp.zeros((8, 128), jnp.float32)
    for k in range(ITERS + 1):
        block = block + jnp.where(row == k, jnp.sum(parts[k], axis=0, keepdims=True), 0.0)
    total_out[...] = block
    group = [(0, 0, dy) for dy in range(1, n_y)] if ring else peers
    me = y if ring else x * n_y + y
    total_in[me] = block
    total_copies = [
        remote(total_out, total_in.at[me], total_sems, (number,), 0, dx, dy)
        for number, (_, dx, dy) in enumerate(group)
    ]
    for copy in total_copies:
        copy.start()

    def emit(which, ref, first_row):
        for colour in (0, 1):
            pieces = []
            lanes = lax.broadcasted_iota(jnp.int32, (18, 128), 1)
            for s in range(6):
                v = ref[pl.ds(first_row(colour) * 8 + s + 1, 18, stride=8), :]
                pieces.append(jnp.where(lanes < NZ, v, pltpu.roll(v, 128 - (64 - NZ), 1)))
            for number in range(5):
                value = None
                for s in range(6):
                    start = 2 * NZ * s - 128 * number
                    if start >= 128 or start + 2 * NZ <= 0:
                        continue
                    moved = pltpu.roll(pieces[s], start % 128, 1) if start % 128 else pieces[s]
                    value = moved if value is None else jnp.where(lanes >= start, moved, value)
                out_ref[which, colour, :, number * 128 : number * 128 + 128] = value

    emit(0, field.at[0], lambda colour: colour * COMPS + GAUGE)
    for colour in (0, 1):
        time_copy(colour).wait_recv()
    for colour in (0, 1):
        v = [tile(time_links, colour * 18 + c) for c in range(18)]
        g = [tile(time_in.at[colour], c) for c in range(18)]
        turned = [None] * 18
        add_links_times_dagger(turned, times(matrix(0, colour, GAUGE), v), g)
        for c in range(18):
            rotated[pl.ds((colour * 18 + c) * 8, 8), :] = turned[c]
    emit(1, rotated, lambda colour: colour * 18)

    for copy in first_copies + edge_copies + total_copies:
        copy.wait_send()
    for colour in (0, 1):
        time_copy(colour).wait_send()
    for copy in total_copies:
        copy.wait_recv()
    total = total_in[0]
    for number in range(1, len(group) + 1):
        total = total + total_in[number]
    sums_ref[...] = jnp.broadcast_to(jnp.sum(total, axis=1, keepdims=True), (8, 128))


def local(space_links, time_links, start_gauge):
    n_t, n_x, n_y = (lax.axis_size(a) for a in ("ta", "gx", "gy"))
    planes, width = start_gauge.shape[4], start_gauge.shape[5]
    assert start_gauge.shape[3] == 1 and planes == 2 and width == 12 * NZ
    volume = planes * n_x * width * n_y
    ring = n_x == 2
    slots = 2 if ring else 3
    group = n_y if ring else n_x * n_y
    site = jnp.arange(width)
    even = (site // NZ + site % NZ) % 2 == 0

    def packed(a):
        a = a.reshape((-1, planes, width))
        low, high = a[:, 0], a[:, 1]
        return jnp.where(even, low, high), jnp.where(even, high, low)

    links = packed(space_links)
    gauge = packed(start_gauge)
    times_ = packed(time_links)
    wide = (-width) % 128
    raw = jnp.pad(
        jnp.concatenate([links[0], gauge[0], links[1], gauge[1]], axis=0), ((0, 0), (0, wide))
    )
    temporal = jnp.pad(jnp.concatenate(times_, axis=0), ((0, 4), (0, wide)))
    vmem = pl.BlockSpec(memory_space=pltpu.VMEM)
    f32 = jnp.float32
    dma = pltpu.SemaphoreType.DMA
    n_full = 1 if ring else ITERS
    out, sums = pl.pallas_call(
        functools.partial(kernel, (n_t, n_x, n_y)),
        out_shape=(
            jax.ShapeDtypeStruct((2, 2, 18, width + wide), f32),
            jax.ShapeDtypeStruct((8, 128), f32),
        ),
        in_specs=[vmem, vmem],
        out_specs=(vmem, vmem),
        scratch_shapes=[
            pltpu.VMEM((slots - 1, 2 * COMPS, width + wide), f32),
            pltpu.VMEM((slots, 2 * COMPS * 8, 128), f32),
            pltpu.VMEM((slots, 108 * 8, 128), f32),
            pltpu.VMEM((2, 2 * COMPS, 128), f32),
            pltpu.VMEM((slots, 2, 2 * COMPS, 128), f32),
            pltpu.VMEM((ITERS, 2, 2 if ring else 1, 18, 128), f32),
            pltpu.VMEM((ITERS, 1 if ring else 3, 2, 2 if ring else 1, 18, 128), f32),
            pltpu.VMEM((n_full, 2, 144, 128), f32),
            pltpu.VMEM((40 * 8, 128), f32),
            pltpu.VMEM((2, 144, 128), f32),
            pltpu.VMEM((288, 128), f32),
            pltpu.VMEM((ITERS + 1, 8, 128), f32),
            pltpu.VMEM((8, 128), f32),
            pltpu.VMEM((group, 8, 128), f32),
            dma((2, slots - 1)),
            dma((2, slots, 2)),
            dma((2, ITERS, 1 if ring else 3, 2)),
            dma((2, n_full, 2)),
            dma((2, 2)),
            dma((2, group - 1)),
        ],
        compiler_params=pltpu.CompilerParams(collective_id=0, has_side_effects=True),
    )(raw, temporal)

    def unpacked(a):
        first, second = a[0, :, :width], a[1, :, :width]
        both = jnp.stack([jnp.where(even, first, second), jnp.where(even, second, first)], axis=1)
        return both.reshape((2, 3, 3, 1, planes, width))

    functional = sums[:ITERS, :1] / (9.0 * volume)
    theta = sums[ITERS, :1] / (3.0 * volume)
    return (unpacked(out[0]), unpacked(out[1]), functional, theta)


def solution(mesh):
    field = P(None, None, None, "ta", "gx", "gy")
    return jax.shard_map(
        local,
        mesh=mesh,
        in_specs=(P(None, None, None, None, "ta", "gx", "gy"), field, field),
        out_specs=(field, field, P(None, "ta"), P("ta")),
        check_vma=False,
    )
```

profile of v0, /device:TPU:0, one launch (start us, length us, event | category | flops | bytes accessed | tf_op | source)
XLA Modules:
  0.0 56.6 jit_solution(15365998209919062471)
XLA Ops:
  0.7 1.2 %fusion.19 = (f32[18,1,576]{2,1,0:T(1,128)S(1)}, f32[18,1,576]{2,1,0:T(1,128)S(1)}, f32[18,1,576]{2,1,0:T(1,128)S(1)}, f32[18,1,576]{2,1,0:T(1,128)S(1)}) fusion(f32[18,2,576]{2,1,0:T(2,128)} %bitcast.45, f32[18,2,576]{2,1,0:T(2,128)} %bitcast.46), kind=kLoop, calls=%fused_computation.48 | loop fusion | bytes 331776 | tf_op jit(solution)/shard_map/slice | solution.py:415
  1.8 0.0 copy-start
  1.9 0.7 %select_maximum_fusion.3.time_ref = f32[40,640]{1,0:T(8,128)} fusion(f32[18,576]{1,0:T(8,128)S(1)} %get-tuple-element.31, f32[18,576]{1,0:T(8,128)S(1)} %get-tuple-element.30), kind=kLoop, calls=%fused_computation.10 | loop fusion | flops 204800 | bytes 185344 | tf_op jit(solution)/shard_map/concatenate | solution.py:425
  2.6 0.3 copy-done
  2.8 0.2 fusion.16
  3.1 0.8 %select_maximum_fusion.raw_ref = f32[144,640]{1,0:T(8,128)} fusion(f32[18,576]{1,0:T(8,128)S(1)} %get-tuple-element.40, f32[54,576]{1,0:T(8,128)S(1)} %get-tuple-element.17, f32[18,576]{1,0:T(8,128)S(1)} %get-tuple-element.41, f32[54,576]{1,0:T(8,128)S(1)} %get-tuple-element.16), kind=kLoop, calls=%fused_computation | loop fusion | flops 737280 | bytes 700416 | tf_op jit(solution)/shard_map/concatenate | solution.py:423
  3.9 45.6 %shard_map.66 = (f32[2,2,18,640]{3,2,1,0:T(8,128)}, f32[8,128]{1,0:T(8,128)}) custom-call(f32[144,640]{1,0:T(8,128)} %select_maximum_fusion.raw_ref, f32[40,640]{1,0:T(8,128)} %select_maximum_fusion.3.time_ref), custom_call_target="tpu_custom_call" | custom-call | tf_op jit(solution)/shard_map/pallas_call | solution.py:430
  49.5 1.2 %slice.55 = f32[1,1]{1,0:T(1,128)} slice(f32[8,128]{1,0:T(8,128)} %get-tuple-element.7), slice={[4:5], [0:1]} | slice | bytes 8 | tf_op jit(solution)/shard_map/slice | solution.py:469
  51.3 1.0 %slice_bitcast_fusion = (f32[2,18,640]{2,1,0:T(8,128)S(1)}, f32[2,18,640]{2,1,0:T(8,128)S(1)}) fusion(f32[2,2,18,640]{3,2,1,0:T(8,128)} %get-tuple-element.6), kind=kLoop, calls=%fused_computation.8 | loop fusion | bytes 368640 | tf_op jit(solution)/shard_map/squeeze | solution.py:470
  52.3 0.0 copy-start.1
  52.4 0.6 %copy-done.1 = f32[8,128]{1,0:T(8,128)S(1)} copy-done((f32[8,128]{1,0:T(8,128)S(1)}, f32[8,128]{1,0:T(8,128)}, u32[]{:S(2)}) %copy-start.1) | copy-done | bytes 4120
  53.0 0.6 %copy.27 = f32[4,1]{0,1:T(1,128)} copy(f32[4,1]{1,0:T(4,128)S(1)} %slice_multiply_fusion) | data formatting | bytes 32
  53.8 0.1 broadcast_select_fusion.1
  53.9 0.1 pad_maximum_fusion.1
  54.0 0.7 %copy.26 = f32[2,3,3,1,2,576]{5,4,3,2,1,0:T(2,128)} copy(f32[2,3,3,1,2,576]{5,3,2,1,0,4:T(1,128)S(1)} %pad_maximum_fusion.1) | data formatting | bytes 165888
  54.7 0.1 pad_maximum_fusion
  54.8 0.7 %copy.25 = f32[2,3,3,1,2,576]{5,4,3,2,1,0:T(2,128)} copy(f32[2,3,3,1,2,576]{5,3,2,1,0,4:T(1,128)S(1)} %pad_maximum_fusion) | data formatting | bytes 165888
  (10 shorter events, 0.3 us)
Async XLA Ops:
  1.8 1.0 %copy-start = (f32[3,2,3,3,1,2,576]{6,5,4,3,2,1,0:T(2,128)S(1)}, f32[3,2,3,3,1,2,576]{6,5,4,3,2,1,0:T(2,128)}, u32[]{:S(2)}) copy-start(f32[3,2,3,3,1,2,576]{6,5,4,3,2,1,0:T(2,128)} %param.3) | copy-start | bytes 746500
  52.3 0.7 %copy-start.1 = (f32[8,128]{1,0:T(8,128)S(1)}, f32[8,128]{1,0:T(8,128)}, u32[]{:S(2)}) copy-start(f32[8,128]{1,0:T(8,128)} %get-tuple-element.7) | copy-start | bytes 12292
where the time goes:
time: 56.9 us; the launch traced here: 56.6 us
  Pallas kernels  45.6 us (80%)
  local copies, waits for them, and re-layouts  6.63 us (12%)
  between operations  2.53 us (4%)
  other arithmetic  1.81 us (3%)
    pallas_call x1, Pallas kernels, local(): pl.pallas_call(functools.partial(kernel, (n_t, n_x, n_y)), out_shape=(jax...  45.6 us
    unnamed x7, local copies, waits for them, and re-layouts  2.87 us
    slice x2, local copies, waits for them, and re-layouts, packed(): low, high = (a[:, 0], a[:, 1])  1.41 us
    slice x1, local copies, waits for them, and re-layouts, local(): theta = sums[ITERS, :1] / (3.0 * volume)  1.18 us

commit v1 on v0

--- a/solution.py
+++ b/solution.py
@@ -13,8 +13,7 @@
 FLOOR = 0.5
 PAIRS = ((0, 1), (1, 2), (0, 2))
 
-COMPS = 72
-GAUGE = 54
+SENT = 48
 MESH = pl.DeviceIdType.MESH
 
 
@@ -124,10 +123,10 @@
 
 
 def kernel(
-    sizes, raw_ref, time_ref, out_ref, sums_ref,
-    raw_in, field, back, edge_out, edge_in, step_out, step_in, full_in,
+    sizes, links_ref, gauge_ref, time_ref, out_ref, sums_ref,
+    raw, flat, time_raw, time_flat, field, gauge, back, edge_out, edge_in, step_out, step_in, full_in,
     time_links, time_in, rotated, parts, total_out, total_in,
-    raw_sems, edge_sems, step_sems, full_sems, time_sems, total_sems,
+    local_sems, raw_sems, edge_sems, step_sems, full_sems, time_sems, total_sems,
 ):
     n_t, n_x, n_y = sizes
     ring = n_x == 2
@@ -154,8 +153,17 @@
             device_id_type=MESH,
         )
 
+    local_copies = [
+        pltpu.make_async_copy(links_ref.at[:, pl.ds(0, 6)], raw.at[0, pl.ds(0, 6)], local_sems.at[0]),
+        pltpu.make_async_copy(gauge_ref.at[:, pl.ds(0, 6)], raw.at[0, pl.ds(6, 2)], local_sems.at[1]),
+        pltpu.make_async_copy(time_ref, time_raw, local_sems.at[2]),
+    ]
+    for copy in local_copies:
+        copy.start()
     peers = [(0, dx, dy) for dx in range(n_x) for dy in range(n_y) if dx or dy]
-    greet = peers + [(1, 0, 0), (n_t - 1, 0, 0)]
+    group = [(0, 0, dy) for dy in range(1, n_y)] if ring else peers
+    near = [(0, d, dy) for d in offsets for dy in (0, 1, n_y - 1) if d or dy]
+    greet = sorted(set(group + near + [(1, 0, 0), (n_t - 1, 0, 0)]))
     barrier = pltpu.get_barrier_semaphore()
     for peer in greet:
         pl.semaphore_signal(barrier, inc=1, device_id=device(*peer), device_id_type=MESH)
@@ -182,22 +190,44 @@
 
         return jnp.where(lanes < 64, window(off), window(off + NZ - 64))
 
-    rows = 2 * COMPS
+    rows = 2 * SENT
     last = 6
-    edge_low = spread_row(raw_ref, rows, 0)
-    edge_high = spread_row(raw_ref, rows, last - 1)
-    edge_out[0] = edge_low
-    edge_out[1] = edge_high
-    own = field.at[0]
-    own[pl.ds(1, rows, stride=8), :] = edge_low
-    own[pl.ds(last, rows, stride=8), :] = edge_high
+
+    def flatten(source, target, count):
+        for number in range(5):
+            lanes = min(128, 12 * NZ - 128 * number)
+            at = slice(128 * number, 128 * number + lanes)
+            site = 128 * number + lax.broadcasted_iota(jnp.int32, (count, 128), 1)
+            even = lax.rem(lax.div(site, NZ) + lax.rem(site, NZ), 2) == 0
+            planes = [source[:, plane, at] for plane in (0, 1)]
+            if lanes < 128:
+                planes = [jnp.concatenate([v, v], axis=1) for v in planes]
+            whole = slice(128 * number, 128 * number + 128)
+            target[0:count, whole] = jnp.where(even, planes[0], planes[1])
+            target[count : 2 * count, whole] = jnp.where(even, planes[1], planes[0])
 
     pl.semaphore_wait(barrier, len(greet))
     first_copies = []
     for p, d in enumerate(offsets):
         if d:
-            first_copies.append(remote(raw_ref, raw_in.at[p - 1], raw_sems, (p - 1,), 0, -d, 0))
-            first_copies[-1].start()
+            first_copies.append(
+                remote(
+                    gauge_ref.at[:, pl.ds(0, 6)], raw.at[p, pl.ds(6, 2)], raw_sems, (p - 1, 1), 0, -d, 0
+                )
+            )
+            first_copies.append(
+                remote(
+                    links_ref.at[:, pl.ds(0, 6)], raw.at[p, pl.ds(0, 6)], raw_sems, (p - 1, 0), 0, -d, 0
+                )
+            )
+    for copy in local_copies:
+        copy.wait()
+    own = field.at[0]
+    flatten(raw.at[0].reshape(SENT, 2, 12 * NZ), flat, SENT)
+    for way, s in ((0, 0), (1, last - 1)):
+        edge = spread_row(flat, rows, s)
+        edge_out[way] = edge
+        own[pl.ds(s + 1, rows, stride=8), :] = edge
     edge_copies = []
     for p, d in enumerate(offsets):
         for way in (0, 1):
@@ -205,66 +235,107 @@
                 remote(edge_out.at[way], edge_in.at[p, way], edge_sems, (p, way), 0, -d, (-1, 1)[way])
             )
             edge_copies[-1].start()
+    for copy in first_copies:
+        copy.start()
 
     for s in range(1, last - 1):
-        own[pl.ds(s + 1, rows, stride=8), :] = spread_row(raw_ref, rows, s)
+        own[pl.ds(s + 1, rows, stride=8), :] = spread_row(flat, rows, s)
+    flatten(time_raw, time_flat, 18)
     for s in range(6):
-        time_links[pl.ds(s + 1, 40, stride=8), :] = spread_row(time_ref, 40, s)
+        time_links[pl.ds(s + 1, 36, stride=8), :] = spread_row(time_flat, 36, s)
     for copy in first_copies:
         copy.wait_recv()
     for p in range(1, slots):
+        flatten(raw.at[p].reshape(SENT, 2, 12 * NZ), flat, SENT)
         for s in range(last):
-            field.at[p][pl.ds(s + 1, rows, stride=8), :] = spread_row(raw_in.at[p - 1], rows, s)
+            field.at[p][pl.ds(s + 1, rows, stride=8), :] = spread_row(flat, rows, s)
     for copy in edge_copies:
         copy.wait_recv()
     for p in range(slots):
         field.at[p][pl.ds(7, rows, stride=8), :] = edge_in[p, 0]
         field.at[p][pl.ds(0, rows, stride=8), :] = edge_in[p, 1]
 
-    def matrix(p, colour, base):
-        return [tile(field.at[p], colour * COMPS + base + c) for c in range(18)]
-
-    def neighbour(p, colour, base, c, direction, step):
-        at = (1 - colour) * COMPS + base + c
-        here = tile(field.at[p], at)
+    def link_row(colour, which, c):
+        part, inner = divmod(c, 9)
+        if inner < 6:
+            return colour * SENT + (which * 2 + part) * 6 + inner
+        return rows + colour * 18 + (which * 2 + part) * 3 + inner - 6
+
+    def put(ref, p, at, value):
+        ref[p, pl.ds(at * 8, 8), :] = value
+
+    for p in range(slots):
+        for colour in (0, 1):
+            for which in range(4):
+                m = [None] * 18
+                for c in range(18):
+                    if c % 9 < 6:
+                        m[c] = tile(field.at[p], link_row(colour, which, c))
+                for k in range(3):
+                    i, j = (k + 1) % 3, (k + 2) % 3
+                    ar, ai, br, bi = m[i], m[9 + i], m[3 + j], m[12 + j]
+                    cr, ci, dr, di = m[j], m[9 + j], m[3 + i], m[12 + i]
+                    m[6 + k] = (ar * br - ai * bi) - (cr * dr - ci * di)
+                    m[15 + k] = (cr * di + ci * dr) - (ar * bi + ai * br)
+                for c in range(18):
+                    if which == 3:
+                        put(gauge, p, colour * 18 + c, m[c])
+                    elif c % 9 >= 6:
+                        put(field, p, link_row(colour, which, c), m[c])
+
+    def links(p, colour, which):
+        return [tile(field.at[p], link_row(colour, which, c)) for c in range(18)]
+
+    def matrix(p, colour):
+        return [tile(gauge.at[p], colour * 18 + c) for c in range(18)]
+
+    def neighbour(ref, p, colour, at, direction, step):
+        here = tile(ref.at[p], at)
         if direction == 2:
             return z_shift(here, masks, step)
         if direction == 1:
             return y_shift(here, masks, step)
         if step > 0:
-            return jnp.where(first_plane[colour], here, tile(field.at[ahead[p]], at))
-        return jnp.where(first_plane[colour], tile(field.at[behind[p]], at), here)
+            return jnp.where(first_plane[colour], here, tile(ref.at[ahead[p]], at))
+        return jnp.where(first_plane[colour], tile(ref.at[behind[p]], at), here)
 
     for p in range(slots):
         for direction in range(3):
             for colour in (0, 1):
                 for c in range(18):
-                    value = neighbour(p, colour, direction * 18, c, direction, -1)
-                    back[p, pl.ds((((direction * 2) + colour) * 18 + c) * 8, 8), :] = value
+                    value = neighbour(
+                        field, p, colour, link_row(1 - colour, direction, c), direction, -1
+                    )
+                    put(back, p, (direction * 2 + colour) * 18 + c, value)
+
+    def around(p, colour, direction, step):
+        return [
+            neighbour(gauge, p, colour, (1 - colour) * 18 + c, direction, step) for c in range(18)
+        ]
 
     def staple(p, colour):
         total = [None] * 18
         for direction in range(3):
-            u = matrix(p, colour, direction * 18)
-            g = [neighbour(p, colour, GAUGE, c, direction, 1) for c in range(18)]
+            u = links(p, colour, direction)
+            g = around(p, colour, direction, 1)
             add_links_times_dagger(total, u, g)
             v = [tile(back.at[p], (direction * 2 + colour) * 18 + c) for c in range(18)]
-            g = [neighbour(p, colour, GAUGE, c, direction, -1) for c in range(18)]
+            g = around(p, colour, direction, -1)
             add_dagger_times_dagger(total, v, g)
         return total
 
     def half(p, colour):
-        g, m = relax(matrix(p, colour, GAUGE), times(matrix(p, colour, GAUGE), staple(p, colour)))
+        g, m = relax(matrix(p, colour), times(matrix(p, colour), staple(p, colour)))
         return g, m
 
     def store(p, colour, g):
         for c in range(18):
-            field[p, pl.ds((colour * COMPS + GAUGE + c) * 8, 8), :] = g[c]
+            put(gauge, p, colour * 18 + c, g[c])
 
     summed = range(slots) if ring else range(1)
 
     def gauge_rows(p, colour):
-        return field.at[p, pl.ds((colour * COMPS + GAUGE) * 8, 18 * 8), :]
+        return gauge.at[p, pl.ds(colour * 144, 144), :]
 
     def time_copy(colour):
         return remote(gauge_rows(0, colour), time_in.at[colour], time_sems, (colour,), -1, 0, 0)
@@ -314,10 +385,10 @@
                 square = two if square is None else square + two
         parts[k] = jnp.where(counted, trace, 0.0)
         parts[ITERS] = jnp.where(counted, square, 0.0)
-        base = (COMPS + GAUGE) * 8
+        base = 144
         for p in summed:
             for way in (0, 1):
-                edge = field.at[p][pl.ds(base + (1, last)[way], 18, stride=8), :]
+                edge = gauge.at[p][pl.ds(base + (1, last)[way], 18, stride=8), :]
                 step_out[k, way, p] = edge
         copies = step_copies(k)
         for copy in copies:
@@ -329,11 +400,11 @@
             copy.wait_recv()
         if not ring:
             for p in range(1, slots):
-                field[p, pl.ds(base, 144), :] = full_in[k, p - 1]
+                gauge[p, pl.ds(base, 144), :] = full_in[k, p - 1]
         for p in range(slots):
             source = (0, p) if ring else (p, 0)
-            field.at[p][pl.ds(base + 7, 18, stride=8), :] = step_in[k, source[0], 0, source[1]]
-            field.at[p][pl.ds(base, 18, stride=8), :] = step_in[k, source[0], 1, source[1]]
+            gauge.at[p][pl.ds(base + 7, 18, stride=8), :] = step_in[k, source[0], 0, source[1]]
+            gauge.at[p][pl.ds(base, 18, stride=8), :] = step_in[k, source[0], 1, source[1]]
         return carry
 
     lax.fori_loop(0, ITERS, iteration, 0)
@@ -341,14 +412,13 @@
 
     square = None
     for p in summed:
-        two = squares(times(matrix(p, 0, GAUGE), staple(p, 0)))
+        two = squares(times(matrix(p, 0), staple(p, 0)))
         square = two if square is None else square + two
     parts[ITERS] = parts[ITERS] + jnp.where(counted, square, 0.0)
     block = jnp.zeros((8, 128), jnp.float32)
     for k in range(ITERS + 1):
         block = block + jnp.where(row == k, jnp.sum(parts[k], axis=0, keepdims=True), 0.0)
     total_out[...] = block
-    group = [(0, 0, dy) for dy in range(1, n_y)] if ring else peers
     me = y if ring else x * n_y + y
     total_in[me] = block
     total_copies = [
@@ -375,14 +445,14 @@
                     value = moved if value is None else jnp.where(lanes >= start, moved, value)
                 out_ref[which, colour, :, number * 128 : number * 128 + 128] = value
 
-    emit(0, field.at[0], lambda colour: colour * COMPS + GAUGE)
+    emit(0, gauge.at[0], lambda colour: colour * 18)
     for colour in (0, 1):
         time_copy(colour).wait_recv()
     for colour in (0, 1):
         v = [tile(time_links, colour * 18 + c) for c in range(18)]
         g = [tile(time_in.at[colour], c) for c in range(18)]
         turned = [None] * 18
-        add_links_times_dagger(turned, times(matrix(0, colour, GAUGE), v), g)
+        add_links_times_dagger(turned, times(matrix(0, colour), v), g)
         for c in range(18):
             rotated[pl.ds((colour * 18 + c) * 8, 8), :] = turned[c]
     emit(1, rotated, lambda colour: colour * 18)
@@ -399,6 +469,23 @@
     sums_ref[...] = jnp.broadcast_to(jnp.sum(total, axis=1, keepdims=True), (8, 128))
 
 
+def finish(volume, packed_ref, sums_ref, gauge_ref, time_ref, functional_ref, theta_ref):
+    for which, ref in enumerate((gauge_ref, time_ref)):
+        for number in range(5):
+            lanes = min(128, 12 * NZ - 128 * number)
+            at = slice(128 * number, 128 * number + lanes)
+            site = 128 * number + lax.broadcasted_iota(jnp.int32, (18, lanes), 1)
+            even = lax.rem(lax.div(site, NZ) + lax.rem(site, NZ), 2) == 0
+            first, second = (packed_ref[which, colour, :, at] for colour in (0, 1))
+            ref[:, 0, at] = jnp.where(even, first, second)
+            ref[:, 1, at] = jnp.where(even, second, first)
+    lane = lax.broadcasted_iota(jnp.int32, (8, 128), 1)
+    row = lax.broadcasted_iota(jnp.int32, (8, 128), 0)
+    along = jnp.sum(jnp.where(lane == row, sums_ref[...], 0.0), axis=0, keepdims=True)
+    functional_ref[...] = along[:, :ITERS] * (1.0 / (9.0 * volume))
+    theta_ref[...] = sums_ref[ITERS : ITERS + 1, 0:1] * (1.0 / (3.0 * volume))
+
+
 def local(space_links, time_links, start_gauge):
     n_t, n_x, n_y = (lax.axis_size(a) for a in ("ta", "gx", "gy"))
     planes, width = start_gauge.shape[4], start_gauge.shape[5]
@@ -407,50 +494,41 @@
     ring = n_x == 2
     slots = 2 if ring else 3
     group = n_y if ring else n_x * n_y
-    site = jnp.arange(width)
-    even = (site // NZ + site % NZ) % 2 == 0
-
-    def packed(a):
-        a = a.reshape((-1, planes, width))
-        low, high = a[:, 0], a[:, 1]
-        return jnp.where(even, low, high), jnp.where(even, high, low)
-
-    links = packed(space_links)
-    gauge = packed(start_gauge)
-    times_ = packed(time_links)
-    wide = (-width) % 128
-    raw = jnp.pad(
-        jnp.concatenate([links[0], gauge[0], links[1], gauge[1]], axis=0), ((0, 0), (0, wide))
-    )
-    temporal = jnp.pad(jnp.concatenate(times_, axis=0), ((0, 4), (0, wide)))
+    wide = width + (-width) % 128
     vmem = pl.BlockSpec(memory_space=pltpu.VMEM)
+    anywhere = pl.BlockSpec(memory_space=pl.ANY)
     f32 = jnp.float32
     dma = pltpu.SemaphoreType.DMA
     n_full = 1 if ring else ITERS
-    out, sums = pl.pallas_call(
+    packed, sums = pl.pallas_call(
         functools.partial(kernel, (n_t, n_x, n_y)),
         out_shape=(
-            jax.ShapeDtypeStruct((2, 2, 18, width + wide), f32),
+            jax.ShapeDtypeStruct((2, 2, 18, wide), f32),
             jax.ShapeDtypeStruct((8, 128), f32),
         ),
-        in_specs=[vmem, vmem],
+        in_specs=[anywhere] * 3,
         out_specs=(vmem, vmem),
         scratch_shapes=[
-            pltpu.VMEM((slots - 1, 2 * COMPS, width + wide), f32),
-            pltpu.VMEM((slots, 2 * COMPS * 8, 128), f32),
+            pltpu.VMEM((slots, 8, 6, planes, width), f32),
+            pltpu.VMEM((2 * SENT, wide), f32),
+            pltpu.VMEM((18, planes, width), f32),
+            pltpu.VMEM((36, wide), f32),
+            pltpu.VMEM((slots, (2 * SENT + 36) * 8, 128), f32),
+            pltpu.VMEM((slots, 36 * 8, 128), f32),
             pltpu.VMEM((slots, 108 * 8, 128), f32),
-            pltpu.VMEM((2, 2 * COMPS, 128), f32),
-            pltpu.VMEM((slots, 2, 2 * COMPS, 128), f32),
+            pltpu.VMEM((2, 2 * SENT, 128), f32),
+            pltpu.VMEM((slots, 2, 2 * SENT, 128), f32),
             pltpu.VMEM((ITERS, 2, 2 if ring else 1, 18, 128), f32),
             pltpu.VMEM((ITERS, 1 if ring else 3, 2, 2 if ring else 1, 18, 128), f32),
             pltpu.VMEM((n_full, 2, 144, 128), f32),
-            pltpu.VMEM((40 * 8, 128), f32),
+            pltpu.VMEM((36 * 8, 128), f32),
             pltpu.VMEM((2, 144, 128), f32),
             pltpu.VMEM((288, 128), f32),
             pltpu.VMEM((ITERS + 1, 8, 128), f32),
             pltpu.VMEM((8, 128), f32),
             pltpu.VMEM((group, 8, 128), f32),
-            dma((2, slots - 1)),
+            dma((3,)),
+            dma((2, slots - 1, 2)),
             dma((2, slots, 2)),
             dma((2, ITERS, 1 if ring else 3, 2)),
             dma((2, n_full, 2)),
@@ -458,16 +536,29 @@
             dma((2, group - 1)),
         ],
         compiler_params=pltpu.CompilerParams(collective_id=0, has_side_effects=True),
-    )(raw, temporal)
-
-    def unpacked(a):
-        first, second = a[0, :, :width], a[1, :, :width]
-        both = jnp.stack([jnp.where(even, first, second), jnp.where(even, second, first)], axis=1)
-        return both.reshape((2, 3, 3, 1, planes, width))
-
-    functional = sums[:ITERS, :1] / (9.0 * volume)
-    theta = sums[ITERS, :1] / (3.0 * volume)
-    return (unpacked(out[0]), unpacked(out[1]), functional, theta)
+    )(
+        space_links.reshape((6, 9, planes, width)),
+        start_gauge.reshape((2, 9, planes, width)),
+        time_links.reshape((18, planes, width)),
+    )
+    gauge, rotated, functional, theta = pl.pallas_call(
+        functools.partial(finish, volume),
+        out_shape=(
+            jax.ShapeDtypeStruct((18, planes, width), f32),
+            jax.ShapeDtypeStruct((18, planes, width), f32),
+            jax.ShapeDtypeStruct((1, ITERS), f32),
+            jax.ShapeDtypeStruct((1, 1), f32),
+        ),
+        in_specs=[vmem, vmem],
+        out_specs=(vmem,) * 4,
+    )(packed, sums)
+    shape = start_gauge.shape
+    return (
+        gauge.reshape(shape),
+        rotated.reshape(shape),
+        functional.reshape((ITERS, 1)),
+        theta.reshape((1,)),
+    )
 
 
 def solution(mesh):

time: 56.9 us -> 44.1 us (0.78)
  local copies, waits for them, and re-layouts: 6.63 us -> 0 us
  Pallas kernels: 45.6 us -> 43.3 us
  between operations: 2.53 us -> 0.64 us
  other arithmetic: 1.81 us -> 0 us
    pallas_call x1, Pallas kernels: 45.6 us -> 41.6 us  [local(): pl.pallas_call(functools.partial(kernel, (n_t, n_x, n_y)), out_shape=(jax...]
    unnamed x7 -> x0, local copies, waits for them, and re-layouts: 2.87 us -> none
    slice x5 -> x0, local copies, waits for them, and re-layouts: 2.61 us -> none  [the longest x2 1.41 us: packed(): low, high = (a[:, 0], a[:, 1])]
    pallas_call x0 -> x1, Pallas kernels: none -> 1.71 us  [local(): pl.pallas_call(functools.partial(finish, volume), out_shape=(jax.ShapeDty...]
    concatenate x2 -> x0, other arithmetic: 1.43 us -> none  [the longest x1 0.77 us: local(): jnp.concatenate([links[0], gauge[0], links[1], gauge[1]], axis=0)]
    squeeze x5 -> x0, local copies, waits for them, and re-layouts: 1.15 us -> none  [the longest x1 0.98 us: local(): return (unpacked(out[0]), unpacked(out[1]), functional, theta)]
where the time goes in v1:
time: 44.1 us; the launch traced here: 44 us
  Pallas kernels  43.3 us (98%)
  between operations  0.64 us (1%)
    pallas_call x1, Pallas kernels, local(): pl.pallas_call(functools.partial(kernel, (n_t, n_x, n_y)), out_shape=(jax...  41.6 us
    pallas_call x1, Pallas kernels, local(): pl.pallas_call(functools.partial(finish, volume), out_shape=(jax.ShapeDty...  1.71 us

profile of v1, /device:TPU:0, one launch (start us, length us, event | category | flops | bytes accessed | tf_op | source)
XLA Modules:
  0.0 44.0 jit_solution(3735811579885802782)
XLA Ops:
  0.6 41.6 %shard_map.66 = (f32[2,2,18,640]{3,2,1,0:T(8,128)}, f32[8,128]{1,0:T(8,128)}) custom-call(f32[6,9,2,576]{3,2,1,0:T(2,128)} %bitcast.11, f32[2,9,2,576]{3,2,1,0:T(2,128)} %bitcast.12, f32[18,2,576]{2,1,0:T(2,128)} %bitcast.13), custom_call_target="tpu_custom_call" | custom-call | tf_op jit(solution)/shard_map/pallas_call | solution.py:503
  42.3 1.7 %shard_map.67 = (f32[18,2,576]{2,1,0:T(2,128)}, f32[18,2,576]{2,1,0:T(2,128)}, f32[1,4]{1,0:T(1,128)}, f32[1,1]{1,0:T(1,128)}) custom-call(f32[2,2,18,640]{3,2,1,0:T(8,128)} %get-tuple-element.10.packed_ref, f32[8,128]{1,0:T(8,128)} %get-tuple-element.11.sums_ref), custom_call_target="tpu_custom_call" | custom-call | tf_op jit(solution)/shard_map/pallas_call | solution.py:544

commit v2 on v1

--- a/solution.py
+++ b/solution.py
@@ -206,7 +206,6 @@
             target[0:count, whole] = jnp.where(even, planes[0], planes[1])
             target[count : 2 * count, whole] = jnp.where(even, planes[1], planes[0])
 
-    pl.semaphore_wait(barrier, len(greet))
     first_copies = []
     for p, d in enumerate(offsets):
         if d:
@@ -228,6 +227,7 @@
         edge = spread_row(flat, rows, s)
         edge_out[way] = edge
         own[pl.ds(s + 1, rows, stride=8), :] = edge
+    pl.semaphore_wait(barrier, len(greet))
     edge_copies = []
     for p, d in enumerate(offsets):
         for way in (0, 1):
@@ -340,13 +340,14 @@
     def time_copy(colour):
         return remote(gauge_rows(0, colour), time_in.at[colour], time_sems, (colour,), -1, 0, 0)
 
-    def step_copies(k):
+    def step_copies(k, q):
         copies = []
         if ring:
             for way in (0, 1):
                 copies.append(
                     remote(
-                        step_out.at[k, way], step_in.at[k, 0, way], step_sems, (k, 0, way), 0, 0, (-1, 1)[way]
+                        step_out.at[k, way, q], step_in.at[k, 0, way, q], step_sems, (k, q, way),
+                        0, 0, (-1, 1)[way],
                     )
                 )
         else:
@@ -375,9 +376,19 @@
 
         trace = None
         square = None
+        base = 144
+        copies = []
         for p in range(slots):
             g, m = half(p, 1)
             store(p, 1, g)
+            if p in summed:
+                for way in (0, 1):
+                    edge = gauge.at[p][pl.ds(base + (1, last)[way], 18, stride=8), :]
+                    step_out[k, way, p] = edge
+                started = step_copies(k, p)
+                for copy in started:
+                    copy.start()
+                copies += started
             if p in summed:
                 one = m[0] + m[4] + m[8]
                 trace = one if trace is None else trace + one
@@ -385,15 +396,6 @@
                 square = two if square is None else square + two
         parts[k] = jnp.where(counted, trace, 0.0)
         parts[ITERS] = jnp.where(counted, square, 0.0)
-        base = 144
-        for p in summed:
-            for way in (0, 1):
-                edge = gauge.at[p][pl.ds(base + (1, last)[way], 18, stride=8), :]
-                step_out[k, way, p] = edge
-        copies = step_copies(k)
-        for copy in copies:
-            copy.start()
-
         for copy in copies:
             copy.wait_send()
         for copy in copies:
@@ -530,7 +532,7 @@
             dma((3,)),
             dma((2, slots - 1, 2)),
             dma((2, slots, 2)),
-            dma((2, ITERS, 1 if ring else 3, 2)),
+            dma((2, ITERS, slots, 2)),
             dma((2, n_full, 2)),
             dma((2, 2)),
             dma((2, group - 1)),

time: 44.1 us -> 43.2 us (0.980)
  Pallas kernels: 43.3 us -> 42.4 us
    pallas_call x1, Pallas kernels: 41.6 us -> 40.7 us  [local(): pl.pallas_call(functools.partial(kernel, (n_t, n_x, n_y)), out_shape=(jax...]
where the time goes in v2:
time: 43.2 us; the launch traced here: 43.1 us
  Pallas kernels  42.4 us (98%)
  between operations  0.64 us (1%)
    pallas_call x1, Pallas kernels, local(): pl.pallas_call(functools.partial(kernel, (n_t, n_x, n_y)), out_shape=(jax...  40.7 us
    pallas_call x1, Pallas kernels, local(): pl.pallas_call(functools.partial(finish, volume), out_shape=(jax.ShapeDty...  1.71 us

profile of v2, /device:TPU:0, one launch (start us, length us, event | category | flops | bytes accessed | tf_op | source)
XLA Modules:
  0.0 43.1 jit_solution(16264420660581457099)
XLA Ops:
  0.6 40.7 %shard_map.66 = (f32[2,2,18,640]{3,2,1,0:T(8,128)}, f32[8,128]{1,0:T(8,128)}) custom-call(f32[6,9,2,576]{3,2,1,0:T(2,128)} %bitcast.11, f32[2,9,2,576]{3,2,1,0:T(2,128)} %bitcast.12, f32[18,2,576]{2,1,0:T(2,128)} %bitcast.13), custom_call_target="tpu_custom_call" | custom-call | tf_op jit(solution)/shard_map/pallas_call | solution.py:505
  41.4 1.7 %shard_map.67 = (f32[18,2,576]{2,1,0:T(2,128)}, f32[18,2,576]{2,1,0:T(2,128)}, f32[1,4]{1,0:T(1,128)}, f32[1,1]{1,0:T(1,128)}) custom-call(f32[2,2,18,640]{3,2,1,0:T(8,128)} %get-tuple-element.10.packed_ref, f32[8,128]{1,0:T(8,128)} %get-tuple-element.11.sums_ref), custom_call_target="tpu_custom_call" | custom-call | tf_op jit(solution)/shard_map/pallas_call | solution.py:546
